TPU v7x, 32 devices: a whole 2x2x4 slice. The times are simulated.
32 devices in a mesh: group: 8 (over y, x, core), ep: 4 (over z).
Axes of the slice: x: 2, y: 2, z: 4, core: 2. Of those that a mesh axis runs over, the one named last changes fastest.
Arguments:
- tokens: bfloat16 [1024, 3584], P(('group', 'ep')), may hold values from -6 to 6
- expert_ids: int32 [1024, 8], P(('group', 'ep')), may hold values from 0 to 31, as said below
- gate_scores: float32 [1024, 8], P(('group', 'ep')), may hold values from 0.05 to 0.35
- replica_pick: int32 [1024, 8], P(('group', 'ep')), may hold values from 0 to 8
- replica_hot: int32 [4], replicated, may hold values from 0 to 7
- gate_weight: bfloat16 [32, 3584, 1024], P(('group', 'ep')), may hold values from -0.09375 to 0.09375
- up_weight: bfloat16 [32, 3584, 1024], P(('group', 'ep')), may hold values from -0.09375 to 0.09375
- down_weight: bfloat16 [32, 1024, 3584], P(('group', 'ep')), may hold values from -0.1875 to 0.1875
Outputs:
- mixed: bfloat16 [1024, 3584], P(('group', 'ep'))
- slot_load: float32 [32, 2], P(('group', 'ep'))
Inputs may be any that keep to these rules, and one draw needn't show every extreme that they name: `expert_ids`: each row names 8 different experts; in each aligned block of 16 rows (one micro-batch of one device) no expert is named by more than 5 rows, and the expert replica_hot[c] * 4 + c of each ep index c is named by exactly 5 rows.
All inputs are finite; a program needn't handle non-finite values.
Results may differ from a plain program's by a relative error of at most 0.0057.
Values may be sent and summed in bfloat16 or wider, within the bound.
A program may use at most 128 MiB of HBM per device.

v0:
```python
import jax
import jax.numpy as jnp
from jax import lax
from jax.sharding import PartitionSpec as P


def expert_ffn(inputs, w_gate, w_up, w_down):
    gate_act = jnp.dot(inputs, w_gate, preferred_element_type=jnp.float32)
    up_act = jnp.dot(inputs, w_up, preferred_element_type=jnp.float32)
    hidden = (jax.nn.silu(gate_act) * up_act).astype(jnp.bfloat16)
    return jnp.dot(hidden, w_down, preferred_element_type=jnp.float32).astype(jnp.bfloat16)


def body(
    tokens, expert_ids, gate_scores, replica_pick, replica_hot, gate_weight, up_weight, down_weight
):
    ngroup = lax.axis_size("group")
    ep_count = lax.axis_size("ep")
    device_count = ngroup * ep_count
    own_gate = gate_weight[0]
    own_up = up_weight[0]
    own_down = down_weight[0]
    slot_kinds = 1
    tok_dev, width = tokens.shape
    top_count = expert_ids.shape[1]
    micro_len = tok_dev // 2
    capacity = (micro_len * top_count + device_count - 1) // device_count + 1
    slot_count = slot_kinds * device_count * capacity
    key_range = jnp.arange(slot_kinds * device_count, dtype=jnp.int32)
    load_range = jnp.arange(2 * device_count, dtype=jnp.int32)
    token_range = jnp.arange(micro_len, dtype=jnp.int32)
    load_total = jnp.zeros((2 * device_count,), jnp.float32)
    mixed_parts = []
    for micro_index in range(2):
        lower = micro_index * micro_len
        micro_rows = tokens[lower : lower + micro_len]
        micro_ids = expert_ids[lower : lower + micro_len].reshape(-1)
        micro_picks = replica_pick[lower : lower + micro_len].reshape(-1)
        micro_gates = gate_scores[lower : lower + micro_len]
        column = micro_ids % ep_count
        home_group = micro_ids // ep_count
        replicated = (replica_hot[column] == home_group) & (micro_picks < ngroup)
        is_replica = replicated.astype(jnp.int32)
        load_key = (
            jnp.where(replicated, micro_picks, home_group) * ep_count * 2 + column * 2 + is_replica
        )
        key_table = (micro_ids[:, None] == key_range[None, :]).astype(jnp.int32)
        position = jnp.sum(jnp.cumsum(key_table, axis=0) * key_table, axis=1) - 1
        slot_index = micro_ids * capacity + position
        owner_token = (
            jnp.full((slot_count,), -1, jnp.int32)
            .at[slot_index]
            .set(jnp.arange(micro_ids.shape[0], dtype=jnp.int32) // top_count)
        )
        selector = (owner_token[:, None] == token_range[None, :]).astype(jnp.bfloat16)
        outgoing = jnp.dot(selector, micro_rows, preferred_element_type=jnp.float32).astype(
            jnp.bfloat16
        )
        outgoing = outgoing.reshape(device_count, slot_kinds, capacity, width)
        received = lax.all_to_all(
            outgoing, ("group", "ep"), split_axis=0, concat_axis=0, tiled=True
        )
        sources, kinds, items, _ = received.shape
        primary_out = expert_ffn(received[:, 0].reshape(-1, width), own_gate, own_up, own_down)
        returned = lax.all_to_all(
            primary_out.reshape(sources, 1, items, width),
            ("group", "ep"),
            split_axis=0,
            concat_axis=0,
            tiled=True,
        )
        pair_outs = returned.reshape(slot_count, width)[slot_index]
        pair_outs = pair_outs.reshape(micro_len, top_count, width).astype(jnp.float32)
        mixed_parts.append(
            jnp.sum(micro_gates[:, :, None] * pair_outs, axis=1).astype(jnp.bfloat16)
        )
        load_total = load_total + jnp.sum(
            (load_key[:, None] == load_range[None, :]).astype(jnp.float32), axis=0
        )
    slot_loads = (
        lax.psum_scatter(
            load_total.reshape(device_count, 2), ("group", "ep"), scatter_dimension=0, tiled=True
        )
        / top_count
    )
    return (jnp.concatenate(mixed_parts, axis=0), slot_loads)


def solution(mesh):
    return jax.shard_map(
        body,
        mesh=mesh,
        in_specs=(
            P(("group", "ep"), None),
            P(("group", "ep"), None),
            P(("group", "ep"), None),
            P(("group", "ep"), None),
            P(),
            P(("group", "ep"), None, None),
            P(("group", "ep"), None, None),
            P(("group", "ep"), None, None),
        ),
        out_specs=(P(("group", "ep"), None), P(("group", "ep"), None)),
        check_vma=False,
    )
```

profile of v0, /device:TPU:0, one launch (start us, length us, event | category | flops | bytes accessed | tf_op | source)
XLA Modules:
  0.0 223.1 jit_solution(6537174995756129069)
XLA Ops:
  2.2 1.0 scatter_custom_fusion
  3.2 1.4 convolution_convert_fusion.1
  4.6 1.5 reshape.339
  6.0 7.3 %all-to-all-start = ((bf16[32,1,5,3584]{3,2,1,0:T(8,128)(2,1)}), bf16[32,1,5,3584]{3,2,1,0:T(8,128)(2,1)S(1)}, u32[]{:S(2)}, u32[]{:S(2)}) async-start(bf16[32,1,5,3584]{3,2,1,0:T(8,128)(2,1)} %bitcast.74), calls=%async_computation | async-start | bytes 3670016 | tf_op jit(solution)/shard_map/all_to_all | solution.py:60
  15.6 1.5 reshape.343
  17.1 37.5 %all-to-all-done = bf16[32,1,5,3584]{3,2,1,0:T(8,128)(2,1)S(1)} async-done(((bf16[32,1,5,3584]{3,2,1,0:T(8,128)(2,1)}), bf16[32,1,5,3584]{3,2,1,0:T(8,128)(2,1)S(1)}, u32[]{:S(2)}, u32[]{:S(2)}) %all-to-all-start) | async-done | bytes 1146912 | tf_op jit(solution)/shard_map/all_to_all | solution.py:60
  54.6 4.9 %all-to-all-start.2 = ((bf16[32,1,5,3584]{3,2,1,0:T(8,128)(2,1)}), bf16[32,1,5,3584]{3,2,1,0:T(8,128)(2,1)}, u32[]{:S(2)}, u32[]{:S(2)}) async-start(bf16[32,1,5,3584]{3,2,1,0:T(8,128)(2,1)} %bitcast.75), calls=%async_computation.2 | async-start | bytes 3670016 | tf_op jit(solution)/shard_map/all_to_all | solution.py:60
  60.0 4.4 %fusion.10 = f32[160,1024]{1,0:T(8,128)S(1)} fusion(bf16[160,3584]{1,0:T(8,128)(2,1)S(1)} %reshape_squeeze.6, bf16[1,3584,1024]{2,1,0:T(8,128)(2,1)} %param.13), kind=kOutput, calls=%fused_computation.14 | convolution fusion | flops 1174405120 | bytes 9142272 | tf_op jit(solution)/shard_map/dot_general | solution.py:8
  64.5 7.8 %fusion.12 = bf16[160,3584]{1,0:T(8,128)(2,1)S(1)} fusion(bf16[1,1024,3584]{2,1,0:T(8,128)(2,1)} %param.15, bf16[160,3584]{1,0:T(8,128)(2,1)S(1)} %reshape_squeeze.6, bf16[1,3584,1024]{2,1,0:T(8,128)(2,1)} %param.14, f32[160,1024]{1,0:T(8,128)S(1)} %fusion.10), kind=kOutput, calls=%fused_computation.16 | convolution fusion | flops 2350366720 | bytes 17629184 | tf_op jit(solution)/shard_map/dot_general | solution.py:11
  72.3 1.5 reshape.340
  73.7 27.0 %all-to-all-done.2 = bf16[32,1,5,3584]{3,2,1,0:T(8,128)(2,1)} async-done(((bf16[32,1,5,3584]{3,2,1,0:T(8,128)(2,1)}), bf16[32,1,5,3584]{3,2,1,0:T(8,128)(2,1)}, u32[]{:S(2)}, u32[]{:S(2)}) %all-to-all-start.2) | async-done | bytes 1146912 | tf_op jit(solution)/shard_map/all_to_all | solution.py:60
  100.8 4.8 %all-to-all-start.1 = ((bf16[32,1,5,3584]{3,2,1,0:T(8,128)(2,1)}), bf16[32,1,5,3584]{3,2,1,0:T(8,128)(2,1)S(1)}, u32[]{:S(2)}, u32[]{:S(2)}) async-start(bf16[32,1,5,3584]{3,2,1,0:T(8,128)(2,1)} %bitcast.76), calls=%async_computation.1 | async-start | bytes 3670016 | tf_op jit(solution)/shard_map/all_to_all | solution.py:65
  105.6 1.7 reshape_squeeze.7
  107.3 5.3 %fusion.8 = f32[160,1024]{1,0:T(8,128)} fusion(bf16[160,3584]{1,0:T(8,128)(2,1)S(1)} %reshape_squeeze.7, bf16[1,3584,1024]{2,1,0:T(8,128)(2,1)} %param.13), kind=kOutput, calls=%fused_computation.12 | convolution fusion | flops 1174405120 | bytes 9142272 | tf_op jit(solution)/shard_map/dot_general | solution.py:8
  112.6 9.0 %fusion.15 = bf16[160,3584]{1,0:T(8,128)(2,1)} fusion(bf16[1,1024,3584]{2,1,0:T(8,128)(2,1)} %param.15, bf16[160,3584]{1,0:T(8,128)(2,1)S(1)} %reshape_squeeze.7, bf16[1,3584,1024]{2,1,0:T(8,128)(2,1)} %param.14, f32[160,1024]{1,0:T(8,128)} %fusion.8), kind=kOutput, calls=%fused_computation.17 | convolution fusion | flops 2350366720 | bytes 17629184 | tf_op jit(solution)/shard_map/dot_general | solution.py:11
  121.6 2.5 %reshape.344 = bf16[32,1,5,3584]{3,2,0,1:T(8,128)(2,1)} reshape(bf16[160,3584]{1,0:T(8,128)(2,1)} %fusion.15) | data formatting | bytes 2293760 | tf_op jit(solution)/shard_map/reshape | solution.py:66
  124.1 22.7 %all-to-all-done.1 = bf16[32,1,5,3584]{3,2,1,0:T(8,128)(2,1)S(1)} async-done(((bf16[32,1,5,3584]{3,2,1,0:T(8,128)(2,1)}), bf16[32,1,5,3584]{3,2,1,0:T(8,128)(2,1)S(1)}, u32[]{:S(2)}, u32[]{:S(2)}) %all-to-all-start.1) | async-done | bytes 1146912 | tf_op jit(solution)/shard_map/all_to_all | solution.py:65
  146.8 5.1 %all-to-all-start.3 = ((bf16[32,1,5,3584]{3,2,1,0:T(8,128)(2,1)}), bf16[32,1,5,3584]{3,2,1,0:T(8,128)(2,1)}, u32[]{:S(2)}, u32[]{:S(2)}) async-start(bf16[32,1,5,3584]{3,2,1,0:T(8,128)(2,1)} %bitcast.73), calls=%async_computation.3 | async-start | bytes 3670016 | tf_op jit(solution)/shard_map/all_to_all | solution.py:65
  153.2 2.6 %fusion.46 = (s32[128]{0:T(128)S(1)}, s32[128]{0:T(128)S(1)}) fusion(s32[128]{0:T(128)S(1)} %reshape.346, s32[128,1]{0,1:T(1,128)S(1)} %reshape.338, s32[128]{0:T(128)S(1)} %eq.99, s32[]{:T(128)} %bitcast.13, s32[]{:T(128)} %bitcast.14, s32[]{:T(128)} %bitcast.16, s32[]{:T(128)} %bitcast.15, s32[128]{0:T(128)S(1)} %reshape.347, s32[128]{0:T(128)S(1)} %eq.106, ...), kind=kLoop, calls=%fused_computation.83 | loop fusion | flops 12288 | bytes 4112 | tf_op jit(solution)/shard_map/add | solution.py:45
  156.1 58.8 %all-reduce = f32[32,2]{1,0:T(8,128)S(1)} all-reduce(f32[32,2]{1,0:T(8,128)S(1)} %add.186), channel_id=2, replica_groups=mesh['group'=8,'ep'=4] {'group','ep'}, use_global_device_ids=true, to_apply=%region_10.11.clone | all-reduce | flops 64 | bytes 512
  215.9 2.0 gather_fusion
  218.0 1.7 reshape.345
  219.7 1.1 gather_fusion.1
  220.9 1.5 fusion.18
  (48 shorter events, 7.6 us)
Async XLA Ops:
  6.0 9.0 %copy-start.1 = (bf16[32,3584]{1,0:T(8,128)(2,1)S(1)}, bf16[32,3584]{1,0:T(8,128)(2,1)}, u32[]{:S(2)}) copy-start(bf16[32,3584]{1,0:T(8,128)(2,1)} %param.8) | copy-start | bytes 688132
  6.0 48.6 %all-to-all-start = ((bf16[32,1,5,3584]{3,2,1,0:T(8,128)(2,1)}), bf16[32,1,5,3584]{3,2,1,0:T(8,128)(2,1)S(1)}, u32[]{:S(2)}, u32[]{:S(2)}) async-start(bf16[32,1,5,3584]{3,2,1,0:T(8,128)(2,1)} %bitcast.74), calls=%async_computation | async-start | bytes 3670016 | tf_op jit(solution)/shard_map/all_to_all | solution.py:60
  54.6 46.1 %all-to-all-start.2 = ((bf16[32,1,5,3584]{3,2,1,0:T(8,128)(2,1)}), bf16[32,1,5,3584]{3,2,1,0:T(8,128)(2,1)}, u32[]{:S(2)}, u32[]{:S(2)}) async-start(bf16[32,1,5,3584]{3,2,1,0:T(8,128)(2,1)} %bitcast.75), calls=%async_computation.2 | async-start | bytes 3670016 | tf_op jit(solution)/shard_map/all_to_all | solution.py:60
  100.8 46.1 %all-to-all-start.1 = ((bf16[32,1,5,3584]{3,2,1,0:T(8,128)(2,1)}), bf16[32,1,5,3584]{3,2,1,0:T(8,128)(2,1)S(1)}, u32[]{:S(2)}, u32[]{:S(2)}) async-start(bf16[32,1,5,3584]{3,2,1,0:T(8,128)(2,1)} %bitcast.76), calls=%async_computation.1 | async-start | bytes 3670016 | tf_op jit(solution)/shard_map/all_to_all | solution.py:65
  146.8 5.1 %copy-start.2 = (f32[32,8]{0,1:T(8,128)S(1)}, f32[32,8]{0,1:T(8,128)}, u32[]{:S(2)}) copy-start(f32[32,8]{0,1:T(8,128)} %param.10) | copy-start | bytes 3076
  146.8 5.3 %copy-start.3 = (s32[32,8]{0,1:T(8,128)S(1)}, s32[32,8]{0,1:T(8,128)}, u32[]{:S(2)}) copy-start(s32[32,8]{0,1:T(8,128)} %param.11) | copy-start | bytes 3076
  146.8 5.7 %copy-start.4 = (s32[4]{0:T(128)S(1)}, s32[4]{0:T(128)}, u32[]{:S(2)}) copy-start(s32[4]{0:T(128)} %param.12) | copy-start | bytes 52
  146.8 71.2 %all-to-all-start.3 = ((bf16[32,1,5,3584]{3,2,1,0:T(8,128)(2,1)}), bf16[32,1,5,3584]{3,2,1,0:T(8,128)(2,1)}, u32[]{:S(2)}, u32[]{:S(2)}) async-start(bf16[32,1,5,3584]{3,2,1,0:T(8,128)(2,1)} %bitcast.73), calls=%async_computation.3 | async-start | bytes 3670016 | tf_op jit(solution)/shard_map/all_to_all | solution.py:65
  219.7 1.2 copy-start
where the time goes:
time: 224 us; the launch traced here: 223 us
  waiting for transfers between devices  87.3 us (39%)
  blocking collectives  58.8 us (26%)
  matrix products  28.4 us (13%)
  starting transfers between devices  22.1 us (10%)
  local copies, waits for them, and re-layouts  19.3 us (9%)
  other arithmetic  6.36 us (3%)
    all_to_all x2, waiting for transfers between devices, body(): lax.all_to_all(outgoing, ('group', 'ep'), split_axis=0, concat_axis=0, ti...  64.6 us
    unnamed x1, blocking collectives  58.8 us
    all_to_all x2, waiting for transfers between devices, body(): lax.all_to_all(primary_out.reshape(sources, 1, items, width), ('group', '...  22.7 us
    dot_general x2, matrix products, expert_ffn(): jnp.dot(hidden, w_down, preferred_element_type=jnp.float32)  16.8 us
    all_to_all x2, starting transfers between devices, body(): lax.all_to_all(outgoing, ('group', 'ep'), split_axis=0, concat_axis=0, ti...  12.2 us
    all_to_all x2, starting transfers between devices, body(): lax.all_to_all(primary_out.reshape(sources, 1, items, width), ('group', '...  9.86 us
    dot_general x2, matrix products, expert_ffn(): gate_act = jnp.dot(inputs, w_gate, preferred_element_type=jnp.float32)  9.71 us
  transfers between devices with their start and end apart: 4, of which 3 were waited for; matrix products, arithmetic and copies ran while one was open for 20% of the time, Pallas kernels for 0%

commit v1 on v0

v1 whole, which is shorter than its diff:
```python
import jax
import jax.numpy as jnp
from jax import lax
from jax.sharding import PartitionSpec as P

AXES = ("group", "ep")


def body(
    tokens, expert_ids, gate_scores, replica_pick, replica_hot, gate_weight, up_weight, down_weight
):
    ngroup = lax.axis_size("group")
    ep_count = lax.axis_size("ep")
    device_count = ngroup * ep_count
    group_index = lax.axis_index("group")
    ep_index = lax.axis_index("ep")
    me = group_index * ep_count + ep_index
    tok_dev, width = tokens.shape
    top_count = expert_ids.shape[1]
    micro_len = tok_dev // 2
    most = (micro_len * top_count + device_count - 1) // device_count + 1
    capacity = 2 * most * device_count

    routing = jnp.concatenate(
        [expert_ids.astype(jnp.float32), replica_pick.astype(jnp.float32), gate_scores], axis=1
    )
    routing = lax.all_gather(routing, AXES, axis=0, tiled=True)
    every = lax.all_gather(tokens, AXES, axis=0, tiled=True)
    ids = routing[:, :top_count].astype(jnp.int32)
    picks = routing[:, top_count : 2 * top_count].astype(jnp.int32)
    gates = routing[:, 2 * top_count :]

    hot = replica_hot[ep_index]
    in_column = ids % ep_count == ep_index
    replicated = in_column & (ids // ep_count == hot) & (picks < ngroup)
    primary_load = jnp.sum(((ids == me) & ~replicated).astype(jnp.float32))
    replica_load = jnp.sum((replicated & (picks == group_index)).astype(jnp.float32))
    loads = jnp.stack([primary_load, replica_load])[None, :] / top_count

    chosen = ids == me
    mask = jnp.any(chosen, axis=1)
    scale = jnp.sum(jnp.where(chosen, gates, 0.0), axis=1)
    place = jnp.where(mask, jnp.cumsum(mask.astype(jnp.int32)) - 1, -1)
    spot = place[None, :] == jnp.arange(capacity, dtype=jnp.int32)[:, None]
    select = spot.astype(jnp.bfloat16)
    row_scale = jnp.sum(jnp.where(spot, scale[None, :], 0.0), axis=1)
    picked = jnp.dot(select, every, preferred_element_type=jnp.float32).astype(jnp.bfloat16)
    gate_act = jnp.dot(picked, gate_weight[0], preferred_element_type=jnp.float32)
    up_act = jnp.dot(picked, up_weight[0], preferred_element_type=jnp.float32)
    hidden = (jax.nn.silu(gate_act) * up_act).astype(jnp.bfloat16)
    pair_out = jnp.dot(hidden, down_weight[0], preferred_element_type=jnp.float32)
    scaled = (pair_out * row_scale[:, None]).astype(jnp.bfloat16)
    spread = jnp.dot(select.T, scaled, preferred_element_type=jnp.float32).astype(jnp.bfloat16)
    mixed = lax.psum_scatter(spread, AXES, scatter_dimension=0, tiled=True)
    return mixed, loads


def solution(mesh):
    rows = P(AXES, None)
    return jax.shard_map(
        body,
        mesh=mesh,
        in_specs=(rows, rows, rows, rows, P(), P(AXES, None, None), P(AXES, None, None), P(AXES, None, None)),
        out_specs=(rows, rows),
        check_vma=False,
    )
```

time: 224 us -> 290 us (1.29)
  waiting for transfers between devices: 87.3 us -> 160 us
  starting transfers between devices: 22.1 us -> 0.08 us
  blocking collectives: 58.8 us -> 76.5 us
  local copies, waits for them, and re-layouts: 19.3 us -> 3.07 us
  between operations: 0.91 us -> 14.1 us
    reduce_scatter x0 -> x1, waiting for transfers between devices: none -> 159 us  [body(): mixed = lax.psum_scatter(spread, AXES, scatter_dimension=0, tiled=True)]
    all_to_all x4 -> x0, waiting for transfers between devices: 87.3 us -> none  [the longest x2 64.6 us: body(): lax.all_to_all(outgoing, ('group', 'ep'), split_axis=0, concat_axis=0, ti...]
    all_gather x0 -> x1, blocking collectives: none -> 76.5 us  [body(): routing = lax.all_gather(routing, AXES, axis=0, tiled=True)]
    unnamed x1 -> x0, blocking collectives: 58.8 us -> none
    all_to_all x4 -> x0, starting transfers between devices: 22.1 us -> none  [the longest x2 12.2 us: body(): lax.all_to_all(outgoing, ('group', 'ep'), split_axis=0, concat_axis=0, ti...]
    reshape x10 -> x0, local copies, waits for them, and re-layouts: 9.57 us -> none  [the longest x2 4.02 us: body(): primary_out.reshape(sources, 1, items, width)]
    gather x3 -> x0, local copies, waits for them, and re-layouts: 3.83 us -> none  [the longest x2 3.16 us: body(): pair_outs = returned.reshape(slot_count, width)[slot_index]]
    dot_general x6 -> x4, matrix products: 28.4 us -> 29.6 us  [the longest x1 11.2 us: body(): jnp.dot(hidden, down_weight[0], preferred_element_type=jnp.float32)]
  transfers between devices with their start and end apart: 4 -> 2, of which waited for: 3 -> 1; matrix products, arithmetic and copies ran while one was open for 20% -> 3% of each run, Pallas kernels for 0% -> 0%
where the time goes in v1:
time: 290 us; the launch traced here: 289 us
  waiting for transfers between devices  160 us (55%)
  blocking collectives  76.5 us (26%)
  matrix products  29.6 us (10%)
  between operations  14.1 us (5%)
  other arithmetic  5.94 us (2%)
  local copies, waits for them, and re-layouts  3.07 us (1%)
    reduce_scatter x1, waiting for transfers between devices, body(): mixed = lax.psum_scatter(spread, AXES, scatter_dimension=0, tiled=True)  159 us
    all_gather x1, blocking collectives, body(): routing = lax.all_gather(routing, AXES, axis=0, tiled=True)  76.5 us
    dot_general x1, matrix products, body(): jnp.dot(hidden, down_weight[0], preferred_element_type=jnp.float32)  11.2 us
    dot_general x1, matrix products, body(): jnp.dot(picked, gate_weight[0], preferred_element_type=jnp.float32)  6.68 us
    dot_general x1, matrix products, body(): jnp.dot(select.T, scaled, preferred_element_type=jnp.float32)  6.09 us
  transfers between devices with their start and end apart: 2, of which 1 were waited for; matrix products, arithmetic and copies ran while one was open for 3% of the time, Pallas kernels for 0%

profile of v1, /device:TPU:0, one launch (start us, length us, event | category | flops | bytes accessed | tf_op | source)
XLA Modules:
  0.0 289.5 jit_solution(16672365116198364456)
XLA Ops:
  7.2 0.0 all-gather.3.cloned.1.call-start
  7.2 0.7 all-gather.3.cloned.1.call-update
  7.9 0.0 reduce-scatter.2.cloned.1.call-start
  8.0 0.7 convert_element_type.39
  8.6 0.7 convert_element_type.38
  9.3 0.7 maximum_bitcast_fusion
  10.0 76.5 %all-gather = f32[32,32,24]{1,2,0:T(8,128)S(1)} all-gather(f32[1,32,24]{1,2,0:T(8,128)S(1)} %maximum_bitcast_fusion), channel_id=1, replica_groups=mesh['group'=8,'ep'=4] {'group','ep'}, dimensions={0}, use_global_device_ids=true | all-gather | bytes 101376 | tf_op jit(solution)/shard_map/all_gather | solution.py:27
  86.6 0.1 copy.12
  86.6 0.2 reshape.71
  86.8 1.2 dynamic_slice.3
  88.1 0.7 fusion.30
  88.8 0.3 reduce-window.9
  89.1 0.1 slice.17
  89.2 0.1 slice_reduce_fusion
  89.3 0.7 convert_reduce_fusion
  90.0 0.1 bitcast_select_fusion
  90.1 0.2 select_reduce_fusion
  90.3 5.6 %convolution_convert_fusion.1 = bf16[320,3584]{1,0:T(8,128)(2,1)S(1)} fusion(bf16[1024,3584]{1,0:T(8,128)(2,1)} %all-gather.3.cloned.1.call-done, s32[1024]{0:T(1024)S(1)} %bitcast_select_fusion), kind=kOutput, calls=%fused_computation.9 | convolution fusion | flops 2350284800 | bytes 9637888 | tf_op jit(solution)/shard_map/dot_general | solution.py:47
  95.9 1.4 copy-done
  97.3 6.7 %fusion.4 = f32[320,1024]{1,0:T(8,128)} fusion(bf16[320,3584]{1,0:T(8,128)(2,1)S(1)} %convolution_convert_fusion.1, bf16[1,3584,1024]{2,1,0:T(8,128)(2,1)} %param.13), kind=kOutput, calls=%fused_computation.5 | convolution fusion | flops 2348810240 | bytes 10944512 | tf_op jit(solution)/shard_map/dot_general | solution.py:48
  104.0 11.2 %fusion.9 = bf16[320,3584]{1,0:T(8,128)(2,1)S(1)} fusion(bf16[1,1024,3584]{2,1,0:T(8,128)(2,1)} %param.15, f32[320]{0:T(512)S(1)} %select_reduce_fusion, bf16[320,3584]{1,0:T(8,128)(2,1)} %copy-done, bf16[1,3584,1024]{2,1,0:T(8,128)(2,1)} %param.14, f32[320,1024]{1,0:T(8,128)} %fusion.4), kind=kOutput, calls=%fused_computation.8 | convolution fusion | flops 4701880320 | bytes 20579584 | tf_op jit(solution)/shard_map/dot_general | solution.py:51
  115.2 6.1 %convolution_convert_fusion = bf16[1024,3584]{1,0:T(8,128)(2,1)} fusion(bf16[320,3584]{1,0:T(8,128)(2,1)S(1)} %fusion.9, s32[1024]{0:T(1024)S(1)} %bitcast_select_fusion), kind=kOutput, calls=%fused_computation | convolution fusion | flops 2352807936 | bytes 9637888 | tf_op jit(solution)/shard_map/dot_general | solution.py:53
  121.3 1.8 maximum_multiply_fusion
  123.1 159.5 %reduce-scatter.2.cloned.1.call-done = bf16[32,3584]{1,0:T(8,128)(2,1)} async-done(((bf16[1024,3584]{1,0:T(8,128)(2,1)}), bf16[32,3584]{1,0:T(8,128)(2,1)}) %reduce-scatter.2.cloned.1.call-update) | async-done | bytes 229392 | tf_op jit(solution)/shard_map/reduce_scatter | solution.py:54
  (5 shorter events, 0.1 us)
Async XLA Ops:
  7.2 83.1 %all-gather.3.cloned.1.call-start = ((), (), s32[]{:S(2)}) async-start(), calls=%async_computation.1 | async-start | bytes 7569408 | tf_op jit(solution)/shard_map/all_gather | solution.py:28
  7.9 274.7 %reduce-scatter.2.cloned.1.call-start = ((), (), s32[]{:S(2)}) async-start(), calls=%async_computation.2 | async-start | bytes 7569408 | tf_op jit(solution)/shard_map/reduce_scatter | solution.py:54
  95.9 1.4 copy-start
Sparse Core Ops, SparseCore 0:
  10.8 77.1 all-gather.2
  121.4 161.1 reduce-scatter.1

commit v2 on v1

v2 whole, which is shorter than its diff:
```python
import functools

import jax
import jax.numpy as jnp
from jax import lax
from jax.experimental import pallas as pl
from jax.experimental.pallas import tpu as pltpu
from jax.sharding import PartitionSpec as P

AXES = ("group", "ep")
MESH = pl.DeviceIdType.MESH


def place_of(nplane, nep):
    group = lax.axis_index("group")
    ep = lax.axis_index("ep")
    core = lax.rem(group, 2)
    plane = lax.div(group, 2)

    def plane_peer(step):
        other = lax.rem(plane + step, nplane)
        return other, (other * 2 + core, ep)

    def ep_peer(step):
        other = lax.rem(ep + step, nep)
        return other, (group, other)

    return plane, ep, plane_peer, ep_peer


def greet(nplane, nep, plane_peer, ep_peer):
    barrier = pltpu.get_barrier_semaphore()
    for step in range(1, nplane):
        pl.semaphore_signal(barrier, inc=1, device_id=plane_peer(step)[1], device_id_type=MESH)
    for step in range(1, nep):
        pl.semaphore_signal(barrier, inc=1, device_id=ep_peer(step)[1], device_id_type=MESH)
    pl.semaphore_wait(barrier, nplane + nep - 2)


def gather_kernel(nplane, nep, cut, x_ref, out_ref, own_sem, send_a, recv_a, send_b, recv_b):
    plane, ep, plane_peer, ep_peer = place_of(nplane, nep)
    width = x_ref.shape[1]
    cols_a, cols_b = pl.ds(0, cut), pl.ds(cut, width - cut)
    own = pltpu.make_async_copy(x_ref, out_ref.at[plane, ep], own_sem)
    own.start()
    greet(nplane, nep, plane_peer, ep_peer)
    sends = []

    def copy(src, p, e, cols, send, recv, target):
        return pltpu.make_async_remote_copy(
            src_ref=src.at[:, cols],
            dst_ref=out_ref.at[p, e, :, cols],
            send_sem=send,
            recv_sem=recv.at[p * nep + e],
            device_id=target,
            device_id_type=MESH,
        )

    used = {"a": 0, "b": 0}

    def push(src, p, e, half, target):
        cols, send, recv = (cols_a, send_a, recv_a) if half == "a" else (cols_b, send_b, recv_b)
        made = copy(src, p, e, cols, send.at[used[half]], recv, target)
        used[half] += 1
        made.start()
        sends.append(made)

    def arrived(p, e, half):
        cols, send, recv = (cols_a, send_a, recv_a) if half == "a" else (cols_b, send_b, recv_b)
        copy(out_ref.at[p, e], p, e, cols, send.at[0], recv, ep_peer(1)[1]).wait_recv()

    for step in range(1, nep):
        push(x_ref, plane, ep, "a", ep_peer(step)[1])
    for step in range(1, nplane):
        push(x_ref, plane, ep, "b", plane_peer(step)[1])
    for step in range(1, nplane):
        push(x_ref, plane, ep, "a", plane_peer(step)[1])
    for step in range(1, nep):
        push(x_ref, plane, ep, "b", ep_peer(step)[1])
    for back in range(1, max(nplane, nep)):
        if back < nep:
            source = lax.rem(ep + nep - back, nep)
            arrived(plane, source, "a")
            for step in range(1, nplane):
                push(out_ref.at[plane, source], plane, source, "a", plane_peer(step)[1])
        if back < nplane:
            source = lax.rem(plane + nplane - back, nplane)
            arrived(source, ep, "b")
            for step in range(1, nep):
                push(out_ref.at[source, ep], source, ep, "b", ep_peer(step)[1])
    for p_back in range(nplane):
        for e_back in range(nep):
            p = lax.rem(plane + nplane - p_back, nplane)
            e = lax.rem(ep + nep - e_back, nep)
            if p_back > 0:
                arrived(p, e, "a")
            if e_back > 0:
                arrived(p, e, "b")
    for made in sends:
        made.wait_send()
    own.wait()


def gather_plane(tokens, nplane, nep, cut):
    rows, width = tokens.shape
    count = nplane * nep
    return pl.pallas_call(
        functools.partial(gather_kernel, nplane, nep, cut),
        out_shape=jax.ShapeDtypeStruct((nplane, nep, rows, width), tokens.dtype),
        in_specs=[pl.BlockSpec(memory_space=pltpu.VMEM)],
        out_specs=pl.BlockSpec(memory_space=pltpu.VMEM),
        scratch_shapes=[pltpu.SemaphoreType.DMA(())] + [pltpu.SemaphoreType.DMA((count,))] * 4,
        compiler_params=pltpu.CompilerParams(collective_id=0, has_side_effects=True),
    )(tokens)


def scatter_kernel(
    nplane, nep, cut, part_ref, out_ref,
    land_a1, land_b1, mid_a, mid_b, land_a2, land_b2,
    send_a1, recv_a1, send_b1, recv_b1, send_a2, recv_a2, send_b2, recv_b2,
):
    plane, ep, plane_peer, ep_peer = place_of(nplane, nep)
    width = out_ref.shape[1]
    cols_a, cols_b = pl.ds(0, cut), pl.ds(cut, width - cut)
    greet(nplane, nep, plane_peer, ep_peer)

    def move(src, dst, send, recv, target):
        made = pltpu.make_async_remote_copy(
            src_ref=src, dst_ref=dst, send_sem=send, recv_sem=recv, device_id=target, device_id_type=MESH
        )
        made.start()
        return made

    first_a, first_b = {}, {}
    for item in range(1, max(nplane, nep) + 1):
        if item <= nep:
            e = lax.rem(ep + item, nep)
            for step in range(1, nplane):
                p, target = plane_peer(step)
                spot = (step - 1) * nep + item - 1
                first_a[item, step] = move(
                    part_ref.at[p, e, :, cols_a], land_a1.at[step - 1, item - 1],
                    send_a1.at[spot], recv_a1.at[spot], target,
                )
        if item <= nplane:
            p = lax.rem(plane + item, nplane)
            for step in range(1, nep):
                e, target = ep_peer(step)
                spot = (step - 1) * nplane + item - 1
                first_b[item, step] = move(
                    part_ref.at[p, e, :, cols_b], land_b1.at[step - 1, item - 1],
                    send_b1.at[spot], recv_b1.at[spot], target,
                )
    second_a, second_b = [], []
    for item in range(1, max(nplane, nep) + 1):
        if item <= nep:
            e, target = ep_peer(item)
            total = part_ref[plane, e, :, cols_a].astype(jnp.float32)
            for step in range(1, nplane):
                first_a[item, step].wait_recv()
                total = total + land_a1[step - 1, item - 1].astype(jnp.float32)
            if item < nep:
                mid_a[item - 1] = total.astype(mid_a.dtype)
                second_a.append(
                    move(mid_a.at[item - 1], land_a2.at[item - 1], send_a2.at[item - 1], recv_a2.at[item - 1], target)
                )
            else:
                total_a = total
        if item <= nplane:
            p, target = plane_peer(item)
            total = part_ref[p, ep, :, cols_b].astype(jnp.float32)
            for step in range(1, nep):
                first_b[item, step].wait_recv()
                total = total + land_b1[step - 1, item - 1].astype(jnp.float32)
            if item < nplane:
                mid_b[item - 1] = total.astype(mid_b.dtype)
                second_b.append(
                    move(mid_b.at[item - 1], land_b2.at[item - 1], send_b2.at[item - 1], recv_b2.at[item - 1], target)
                )
            else:
                total_b = total
    for index, made in enumerate(second_a):
        made.wait_recv()
        total_a = total_a + land_a2[index].astype(jnp.float32)
    out_ref[:, cols_a] = total_a.astype(out_ref.dtype)
    for index, made in enumerate(second_b):
        made.wait_recv()
        total_b = total_b + land_b2[index].astype(jnp.float32)
    out_ref[:, cols_b] = total_b.astype(out_ref.dtype)
    for made in list(first_a.values()) + list(first_b.values()) + second_a + second_b:
        made.wait_send()


def scatter_plane(parts, cut):
    nplane, nep, rows, width = parts.shape
    rest = width - cut
    kind = parts.dtype
    dma = pltpu.SemaphoreType.DMA
    pairs_a, pairs_b = (nplane - 1) * nep, (nep - 1) * nplane
    return pl.pallas_call(
        functools.partial(scatter_kernel, nplane, nep, cut),
        out_shape=jax.ShapeDtypeStruct((rows, width), kind),
        in_specs=[pl.BlockSpec(memory_space=pltpu.VMEM)],
        out_specs=pl.BlockSpec(memory_space=pltpu.VMEM),
        scratch_shapes=[
            pltpu.VMEM((nplane - 1, nep, rows, cut), kind),
            pltpu.VMEM((nep - 1, nplane, rows, rest), kind),
            pltpu.VMEM((nep - 1, rows, cut), kind),
            pltpu.VMEM((nplane - 1, rows, rest), kind),
            pltpu.VMEM((nep - 1, rows, cut), kind),
            pltpu.VMEM((nplane - 1, rows, rest), kind),
            dma((pairs_a,)), dma((pairs_a,)), dma((pairs_b,)), dma((pairs_b,)),
            dma((nep - 1,)), dma((nep - 1,)), dma((nplane - 1,)), dma((nplane - 1,)),
        ],
        compiler_params=pltpu.CompilerParams(collective_id=1, has_side_effects=True),
    )(parts)


def body(
    tokens, expert_ids, gate_scores, replica_pick, replica_hot, gate_weight, up_weight, down_weight
):
    ngroup = lax.axis_size("group")
    nep = lax.axis_size("ep")
    nplane = ngroup // 2
    device_count = ngroup * nep
    group_index = lax.axis_index("group")
    ep_index = lax.axis_index("ep")
    core = group_index % 2
    me = group_index * nep + ep_index
    partner = (group_index + 1 - 2 * core) * nep + ep_index
    tok_dev, width = tokens.shape
    top_count = expert_ids.shape[1]
    most = (tok_dev // 2 * top_count + device_count - 1) // device_count + 1
    capacity = 2 * most * nplane * nep
    cut = width // 256 * 128

    routing = jnp.concatenate(
        [expert_ids.astype(jnp.float32), replica_pick.astype(jnp.float32), gate_scores], axis=1
    )
    routing = lax.all_gather(routing, AXES, axis=0, tiled=True)
    every = gather_plane(tokens, nplane, nep, cut).reshape(nplane * nep * tok_dev, width)

    ids = routing[:, :top_count].astype(jnp.int32)
    picks = routing[:, top_count : 2 * top_count].astype(jnp.int32)
    hot = replica_hot[ep_index]
    replicated = (ids % nep == ep_index) & (ids // nep == hot) & (picks < ngroup)
    primary_load = jnp.sum(((ids == me) & ~replicated).astype(jnp.float32))
    replica_load = jnp.sum((replicated & (picks == group_index)).astype(jnp.float32))
    loads = jnp.stack([primary_load, replica_load])[None, :] / top_count

    mine = routing.reshape(nplane, 2, nep * tok_dev, routing.shape[1])
    mine = lax.dynamic_index_in_dim(mine, core, 1, keepdims=False).reshape(-1, routing.shape[1])
    my_ids = mine[:, :top_count].astype(jnp.int32)
    my_gates = mine[:, 2 * top_count :]

    def spots(expert):
        chosen = my_ids == expert
        mask = jnp.any(chosen, axis=1)
        scale = jnp.sum(jnp.where(chosen, my_gates, 0.0), axis=1)
        place = jnp.where(mask, jnp.cumsum(mask.astype(jnp.int32)) - 1, -1)
        spot = place[None, :] == jnp.arange(capacity, dtype=jnp.int32)[:, None]
        return spot, jnp.sum(jnp.where(spot, scale[None, :], 0.0), axis=1)

    spot_me, scale_me = spots(me)
    spot_other, scale_other = spots(partner)
    select = jnp.concatenate([spot_me, spot_other], axis=0).astype(jnp.bfloat16)
    row_scale = jnp.concatenate([scale_me, scale_other], axis=0)
    swap = [(index, index ^ 1) for index in range(ngroup)]

    picked = jnp.dot(select, every, preferred_element_type=jnp.float32).astype(jnp.bfloat16)
    inputs = jnp.concatenate(
        [picked[:capacity], lax.ppermute(picked[capacity:], "group", swap)], axis=0
    )
    gate_act = jnp.dot(inputs, gate_weight[0], preferred_element_type=jnp.float32)
    up_act = jnp.dot(inputs, up_weight[0], preferred_element_type=jnp.float32)
    hidden = (jax.nn.silu(gate_act) * up_act).astype(jnp.bfloat16)
    pair_out = jnp.dot(hidden, down_weight[0], preferred_element_type=jnp.float32).astype(jnp.bfloat16)
    pairs = jnp.concatenate(
        [pair_out[:capacity], lax.ppermute(pair_out[capacity:], "group", swap)], axis=0
    )
    scaled = (pairs.astype(jnp.float32) * row_scale[:, None]).astype(jnp.bfloat16)
    spread = lax.dot_general(
        select, scaled, (((0,), (0,)), ((), ())), preferred_element_type=jnp.float32
    ).astype(jnp.bfloat16)
    mixed = scatter_plane(spread.reshape(nplane, nep, tok_dev, width), cut)
    return mixed, loads


def solution(mesh):
    rows = P(AXES, None)
    weights = P(AXES, None, None)
    return jax.shard_map(
        body,
        mesh=mesh,
        in_specs=(rows, rows, rows, rows, P(), weights, weights, weights),
        out_specs=(rows, rows),
        check_vma=False,
    )
```

time: 290 us -> 222 us (0.77)
  waiting for transfers between devices: 160 us -> 2.79 us
  Pallas kernels: 0 us -> 106 us
  between operations: 14.1 us -> 0.78 us
  blocking collectives: 76.5 us -> 72.9 us
  matrix products: 29.6 us -> 26.5 us
    reduce_scatter x1 -> x0, waiting for transfers between devices: 159 us -> none  [body(): mixed = lax.psum_scatter(spread, AXES, scatter_dimension=0, tiled=True)]
    pallas_call x0 -> x2, Pallas kernels: none -> 106 us  [the longest x1 55.4 us: scatter_plane(): pl.pallas_call(functools.partial(scatter_kernel, nplane, nep, cut), out_s...]
    all_gather x1, blocking collectives: 76.5 us -> 72.9 us  [body(): routing = lax.all_gather(routing, AXES, axis=0, tiled=True)]
  transfers between devices with their start and end apart: 2 -> 2, of which waited for: 1 -> 1; matrix products, arithmetic and copies ran while one was open for 3% -> 2% of each run, Pallas kernels for 0% -> 0%
where the time goes in v2:
time: 222 us; the launch traced here: 221 us
  Pallas kernels  106 us (48%)
  blocking collectives  72.9 us (33%)
  matrix products  26.5 us (12%)
  other arithmetic  6.52 us (3%)
  local copies, waits for them, and re-layouts  5.87 us (3%)
  waiting for transfers between devices  2.79 us (1%)
    all_gather x1, blocking collectives, body(): routing = lax.all_gather(routing, AXES, axis=0, tiled=True)  72.9 us
    pallas_call x1, Pallas kernels, scatter_plane(): pl.pallas_call(functools.partial(scatter_kernel, nplane, nep, cut), out_s...  55.4 us
    pallas_call x1, Pallas kernels, gather_plane(): pl.pallas_call(functools.partial(gather_kernel, nplane, nep, cut), out_sh...  50.2 us
    dot_general x1, matrix products, body(): jnp.dot(hidden, down_weight[0], preferred_element_type=jnp.float32)  11.2 us
    dot_general x1, matrix products, body(): up_act = jnp.dot(inputs, up_weight[0], preferred_element_type=jnp.float32)  6.67 us
    dot_general x1, matrix products, body(): lax.dot_general(select, scaled, (((0,), (0,)), ((), ())), preferred_eleme...  5.25 us
  transfers between devices with their start and end apart: 2, of which 1 were waited for; matrix products, arithmetic and copies ran while one was open for 2% of the time, Pallas kernels for 0%

profile of v2, /device:TPU:0, one launch (start us, length us, event | category | flops | bytes accessed | tf_op | source)
XLA Modules:
  0.0 221.2 jit_solution(11305729636922140416)
XLA Ops:
  0.7 0.7 convert_element_type.54
  1.3 0.7 convert_element_type.55
  2.0 0.7 maximum_bitcast_fusion
  2.7 72.9 %all-gather = f32[32,32,24]{1,2,0:T(8,128)S(1)} all-gather(f32[1,32,24]{1,2,0:T(8,128)S(1)} %maximum_bitcast_fusion), channel_id=1, replica_groups=mesh['group'=8,'ep'=4] {'group','ep'}, dimensions={0}, use_global_device_ids=true | all-gather | bytes 101376 | tf_op jit(solution)/shard_map/all_gather | solution.py:240
  75.7 0.2 reshape.112
  75.8 0.2 dynamic-slice_reduce_fusion
  76.1 0.3 reduce-window.24
  76.7 0.3 reduce-window.16
  77.3 50.2 %shard_map.95 = bf16[4,4,32,3584]{3,2,1,0:T(8,128)(2,1)} custom-call(bf16[32,3584]{1,0:T(8,128)(2,1)} %x_ref.1), custom_call_target="tpu_custom_call" | custom-call | tf_op jit(solution)/shard_map/pallas_call | solution.py:107
  127.6 3.4 %convolution_convert_fusion.1 = bf16[320,3584]{1,0:T(8,128)(2,1)S(1)} fusion(bf16[512,3584]{1,0:T(8,128)(2,1)} %bitcast.42, pred[160,512]{1,0:T(32,128)(4,1)S(1)} %get-tuple-element.14, pred[160,512]{1,0:T(32,128)(4,1)S(1)} %get-tuple-element.15), kind=kOutput, calls=%fused_computation.8 | convolution fusion | flops 1175715840 | bytes 6127616 | tf_op jit(solution)/shard_map/dot_general | solution.py:270
  131.0 0.1 fusion.35
  131.3 2.8 %collective-permute-done = bf16[160,3584]{1,0:T(8,128)(2,1)S(1)} collective-permute-done((bf16[160,3584]{1,0:T(8,128)(2,1)S(1)}, bf16[160,3584]{1,0:T(8,128)(2,1)S(1)}, u32[]{:S(2)}, u32[]{:S(2)}) %collective-permute-start) | collective-permute-done | bytes 1146912 | tf_op jit(solution)/shard_map/ppermute | solution.py:272
  134.1 1.0 copy-done.1
  135.1 6.7 %fusion.2 = f32[320,1024]{1,0:T(8,128)} fusion(bf16[1,3584,1024]{2,1,0:T(8,128)(2,1)} %param.14, bf16[160,3584]{1,0:T(8,128)(2,1)S(1)} %collective-permute-done, bf16[160,3584]{1,0:T(8,128)(2,1)S(1)} %get-tuple-element.10), kind=kOutput, calls=%fused_computation.2 | convolution fusion | flops 2353397760 | bytes 10944512 | tf_op jit(solution)/shard_map/dot_general | solution.py:275
  141.8 11.2 %fusion.6 = bf16[320,3584]{1,0:T(8,128)(2,1)S(1)} fusion(bf16[1,1024,3584]{2,1,0:T(8,128)(2,1)} %param.15, f32[320,1024]{1,0:T(8,128)} %fusion.2, bf16[1,3584,1024]{2,1,0:T(8,128)(2,1)} %param.13, bf16[160,3584]{1,0:T(8,128)(2,1)} %copy-done.1, bf16[160,3584]{1,0:T(8,128)(2,1)} %copy-done), kind=kOutput, calls=%fused_computation.7 | convolution fusion | flops 4705320960 | bytes 20578304 | tf_op jit(solution)/shard_map/dot_general | solution.py:277
  153.0 1.5 fusion.34
  154.6 0.2 reshape.121
  154.8 0.6 dynamic_slice.8
  155.4 1.4 convert_reduce_fusion.1
  156.7 1.9 maximum_multiply_fusion
  158.6 0.2 select_reduce_fusion
  158.8 5.2 %convolution_convert_fusion = bf16[512,3584]{1,0:T(8,128)(2,1)} fusion(bf16[160,3584]{1,0:T(8,128)(2,1)S(1)} %collective-permute-done.1, bf16[160,3584]{1,0:T(8,128)(2,1)} %get-tuple-element.8, f32[320]{0:T(512)S(1)} %pad_maximum_fusion.7, pred[160,512]{1,0:T(32,128)(4,1)S(1)} %get-tuple-element.14, pred[160,512]{1,0:T(32,128)(4,1)S(1)} %get-tuple-element.15), kind=kOutput, calls=%fused_computation.6 | convolution fusion | flops 1183285248 | bytes 6128896 | tf_op jit(solution)/shard_map/dot_general | solution.py:282
  164.1 55.4 %shard_map.96 = bf16[32,3584]{1,0:T(8,128)(2,1)} custom-call(bf16[4,4,32,3584]{3,2,1,0:T(8,128)(2,1)} %bitcast.41), custom_call_target="tpu_custom_call" | custom-call | tf_op jit(solution)/shard_map/pallas_call | solution.py:200
  219.5 1.6 copy.26
  (25 shorter events, 1.2 us)
Async XLA Ops:
  131.2 2.9 %copy-start = (bf16[160,3584]{1,0:T(8,128)(2,1)}, bf16[160,3584]{1,0:T(8,128)(2,1)S(1)}, u32[]{:S(2)}) copy-start(bf16[160,3584]{1,0:T(8,128)(2,1)S(1)} %get-tuple-element.10) | copy-start | bytes 3440644
  131.2 2.9 %collective-permute-start = (bf16[160,3584]{1,0:T(8,128)(2,1)S(1)}, bf16[160,3584]{1,0:T(8,128)(2,1)S(1)}, u32[]{:S(2)}, u32[]{:S(2)}) collective-permute-start(bf16[160,3584]{1,0:T(8,128)(2,1)S(1)} %get-tuple-element.11), channel_id=1, source_target_pairs={{0,4},{4,0},{8,12},{12,8},{16,20},{20,16},{24,28},{28,24},{1,5},{5... | collective-permute-start | bytes 3440648 | tf_op jit(solution)/shard_map/ppermute | solution.py:272
  134.1 1.0 copy-start.1
  153.0 1.8 copy-start.2
  154.5 4.4 %collective-permute-start.1 = (bf16[160,3584]{1,0:T(8,128)(2,1)}, bf16[160,3584]{1,0:T(8,128)(2,1)S(1)}, u32[]{:S(2)}, u32[]{:S(2)}) collective-permute-start(bf16[160,3584]{1,0:T(8,128)(2,1)} %get-tuple-element.9), channel_id=1, source_target_pairs={{0,4},{4,0},{8,12},{12,8},{16,20},{20,16},{24,28},{28,24},{1,5},{5... | collective-permute-start | bytes 3440648 | tf_op jit(solution)/shard_map/ppermute | solution.py:279

commit v3 on v2

--- a/solution.py
+++ b/solution.py
@@ -37,81 +37,210 @@
     pl.semaphore_wait(barrier, nplane + nep - 2)
 
 
-def gather_kernel(nplane, nep, cut, x_ref, out_ref, own_sem, send_a, recv_a, send_b, recv_b):
+def gather_kernel(
+    nplane, nep, cut, x_ref, note_ref, out_ref, notes_ref,
+    own_sem, send_a, recv_a, send_b, recv_b, right_a, left_a, right_b, left_b, note_send, note_recv,
+):
     plane, ep, plane_peer, ep_peer = place_of(nplane, nep)
+    group = lax.axis_index("group")
+    me = group * nep + ep
+    total = 2 * nplane * nep
     width = x_ref.shape[1]
-    cols_a, cols_b = pl.ds(0, cut), pl.ds(cut, width - cut)
-    own = pltpu.make_async_copy(x_ref, out_ref.at[plane, ep], own_sem)
+    cols = {"a": pl.ds(0, cut), "b": pl.ds(cut, width - cut)}
+    recv = {"a": recv_a, "b": recv_b}
+    rights = {"a": right_a, "b": right_b}
+    lefts = {"a": left_a, "b": left_b}
+    own = pltpu.make_async_copy(x_ref, out_ref.at[plane, ep], own_sem.at[0])
     own.start()
-    greet(nplane, nep, plane_peer, ep_peer)
-    sends = []
-
-    def copy(src, p, e, cols, send, recv, target):
+    own_note = pltpu.make_async_copy(note_ref, notes_ref.at[me], own_sem.at[1])
+    own_note.start()
+
+    barrier = pltpu.get_barrier_semaphore()
+    for step in range(1, total):
+        other = lax.rem(me + step, total)
+        pl.semaphore_signal(
+            barrier, inc=1, device_id=(lax.div(other, nep), lax.rem(other, nep)), device_id_type=MESH
+        )
+    pl.semaphore_wait(barrier, total - 1)
+
+    def copy(src, p, e, half, send, target):
         return pltpu.make_async_remote_copy(
-            src_ref=src.at[:, cols],
-            dst_ref=out_ref.at[p, e, :, cols],
+            src_ref=src.at[:, cols[half]],
+            dst_ref=out_ref.at[p, e, :, cols[half]],
             send_sem=send,
-            recv_sem=recv.at[p * nep + e],
+            recv_sem=recv[half].at[p * nep + e],
             device_id=target,
             device_id_type=MESH,
         )
 
+    sends = []
     used = {"a": 0, "b": 0}
 
-    def push(src, p, e, half, target):
-        cols, send, recv = (cols_a, send_a, recv_a) if half == "a" else (cols_b, send_b, recv_b)
-        made = copy(src, p, e, cols, send.at[used[half]], recv, target)
-        used[half] += 1
-        made.start()
-        sends.append(made)
+    def push(src, p, e, half):
+        send = send_a if half == "a" else send_b
+        for step in range(1, nplane):
+            made = copy(src, p, e, half, send.at[used[half]], plane_peer(step)[1])
+            used[half] += 1
+            made.start()
+            sends.append(made)
 
     def arrived(p, e, half):
-        cols, send, recv = (cols_a, send_a, recv_a) if half == "a" else (cols_b, send_b, recv_b)
-        copy(out_ref.at[p, e], p, e, cols, send.at[0], recv, ep_peer(1)[1]).wait_recv()
-
-    for step in range(1, nep):
-        push(x_ref, plane, ep, "a", ep_peer(step)[1])
-    for step in range(1, nplane):
-        push(x_ref, plane, ep, "b", plane_peer(step)[1])
-    for step in range(1, nplane):
-        push(x_ref, plane, ep, "a", plane_peer(step)[1])
-    for step in range(1, nep):
-        push(x_ref, plane, ep, "b", ep_peer(step)[1])
+        copy(out_ref.at[p, e], p, e, half, send_a.at[0], ep_peer(1)[1]).wait_recv()
+
+    def to_right(src, p, e, half):
+        return copy(src, p, e, half, rights[half].at[p * nep + e], (group, lax.rem(ep + 1, nep)))
+
+    def to_left(src, p, e, half):
+        return copy(src, p, e, half, lefts[half].at[p * nep + e], (group, lax.rem(ep + nep - 1, nep)))
+
+    has_right, has_left = ep < nep - 1, ep > 0
+
+    def both_ways(src, p, half):
+        @pl.when(has_right)
+        def _():
+            to_right(src, p, ep, half).start()
+
+        @pl.when(has_left)
+        def _():
+            to_left(src, p, ep, half).start()
+
+    def chain(p, back, half):
+        @pl.when(ep - back >= 0)
+        def _():
+            arrived(p, ep - back, half)
+
+            @pl.when(has_right)
+            def _():
+                to_right(out_ref.at[p, ep - back], p, ep - back, half).start()
+
+        @pl.when(ep + back < nep)
+        def _():
+            arrived(p, ep + back, half)
+
+            @pl.when(has_left)
+            def _():
+                to_left(out_ref.at[p, ep + back], p, ep + back, half).start()
+
+    def chain_end(p, back, half):
+        @pl.when((ep - back >= 0) & has_right)
+        def _():
+            to_right(out_ref.at[p, ep - back], p, ep - back, half).wait_send()
+
+        @pl.when((ep + back < nep) & has_left)
+        def _():
+            to_left(out_ref.at[p, ep + back], p, ep + back, half).wait_send()
+
+    def note(source, step, target):
+        return pltpu.make_async_remote_copy(
+            src_ref=note_ref,
+            dst_ref=notes_ref.at[source],
+            send_sem=note_send.at[step],
+            recv_sem=note_recv.at[source],
+            device_id=(lax.div(target, nep), lax.rem(target, nep)),
+            device_id_type=MESH,
+        )
+
+    both_ways(x_ref, plane, "a")
+    push(x_ref, plane, ep, "b")
+    push(x_ref, plane, ep, "a")
+    both_ways(x_ref, plane, "b")
+    for step in range(1, total):
+        note(me, step, lax.rem(me + step, total)).start()
     for back in range(1, max(nplane, nep)):
         if back < nep:
-            source = lax.rem(ep + nep - back, nep)
-            arrived(plane, source, "a")
-            for step in range(1, nplane):
-                push(out_ref.at[plane, source], plane, source, "a", plane_peer(step)[1])
+            chain(plane, back, "a")
         if back < nplane:
             source = lax.rem(plane + nplane - back, nplane)
             arrived(source, ep, "b")
-            for step in range(1, nep):
-                push(out_ref.at[source, ep], source, ep, "b", ep_peer(step)[1])
-    for p_back in range(nplane):
-        for e_back in range(nep):
-            p = lax.rem(plane + nplane - p_back, nplane)
-            e = lax.rem(ep + nep - e_back, nep)
-            if p_back > 0:
-                arrived(p, e, "a")
-            if e_back > 0:
-                arrived(p, e, "b")
+            both_ways(out_ref.at[source, ep], source, "b")
+        if back < nep:
+            left_in, right_in = ep - back >= 0, ep + back < nep
+
+            @pl.when(left_in)
+            def _():
+                for step in range(1, nplane):
+                    copy(
+                        out_ref.at[plane, ep - back], plane, ep - back, "a",
+                        send_a.at[(nplane - 1) * back + step - 1], plane_peer(step)[1],
+                    ).start()
+
+            @pl.when(right_in)
+            def _():
+                for step in range(1, nplane):
+                    copy(
+                        out_ref.at[plane, ep + back], plane, ep + back, "a",
+                        send_a.at[(nplane - 1) * (nep + back) + step - 1], plane_peer(step)[1],
+                    ).start()
+    for back in range(1, nep):
+        for p_back in range(nplane):
+            chain(lax.rem(plane + nplane - p_back, nplane), back, "b")
+    for p_back in range(1, nplane):
+        p = lax.rem(plane + nplane - p_back, nplane)
+        for e in range(nep):
+            arrived(p, e, "a")
+    for step in range(1, total):
+        source = lax.rem(me + total - step, total)
+        note(source, step, lax.rem(me + 1, total)).wait_recv()
     for made in sends:
         made.wait_send()
+    for back in range(1, nep):
+        @pl.when(ep - back >= 0)
+        def _():
+            for step in range(1, nplane):
+                copy(
+                    out_ref.at[plane, ep - back], plane, ep - back, "a",
+                    send_a.at[(nplane - 1) * back + step - 1], plane_peer(step)[1],
+                ).wait_send()
+
+        @pl.when(ep + back < nep)
+        def _():
+            for step in range(1, nplane):
+                copy(
+                    out_ref.at[plane, ep + back], plane, ep + back, "a",
+                    send_a.at[(nplane - 1) * (nep + back) + step - 1], plane_peer(step)[1],
+                ).wait_send()
+
+    for back in range(nep):
+        for half in ("a", "b"):
+            for p_back in range(nplane if half == "b" else 1):
+                p = lax.rem(plane + nplane - p_back, nplane)
+                if back == 0:
+                    @pl.when(has_right)
+                    def _():
+                        to_right(x_ref, p, ep, half).wait_send()
+
+                    @pl.when(has_left)
+                    def _():
+                        to_left(x_ref, p, ep, half).wait_send()
+                else:
+                    chain_end(p, back, half)
+    for step in range(1, total):
+        note(me, step, lax.rem(me + step, total)).wait_send()
     own.wait()
-
-
-def gather_plane(tokens, nplane, nep, cut):
+    own_note.wait()
+
+
+def gather_plane(tokens, note, nplane, nep, cut):
     rows, width = tokens.shape
     count = nplane * nep
+    dma = pltpu.SemaphoreType.DMA
+    vmem = pl.BlockSpec(memory_space=pltpu.VMEM)
     return pl.pallas_call(
         functools.partial(gather_kernel, nplane, nep, cut),
-        out_shape=jax.ShapeDtypeStruct((nplane, nep, rows, width), tokens.dtype),
-        in_specs=[pl.BlockSpec(memory_space=pltpu.VMEM)],
-        out_specs=pl.BlockSpec(memory_space=pltpu.VMEM),
-        scratch_shapes=[pltpu.SemaphoreType.DMA(())] + [pltpu.SemaphoreType.DMA((count,))] * 4,
+        out_shape=[
+            jax.ShapeDtypeStruct((nplane, nep, rows, width), tokens.dtype),
+            jax.ShapeDtypeStruct((2 * count,) + note.shape, note.dtype),
+        ],
+        in_specs=[vmem, vmem],
+        out_specs=[vmem, vmem],
+        scratch_shapes=[
+            dma((2,)),
+            dma((2 * (nplane - 1) * nep,)), dma((count,)), dma((nplane - 1,)), dma((count,)),
+            dma((count,)), dma((count,)), dma((count,)), dma((count,)),
+            dma((2 * count,)), dma((2 * count,)),
+        ],
         compiler_params=pltpu.CompilerParams(collective_id=0, has_side_effects=True),
-    )(tokens)
+    )(tokens, note)
 
 
 def scatter_kernel(
@@ -233,25 +362,26 @@
     most = (tok_dev // 2 * top_count + device_count - 1) // device_count + 1
     capacity = 2 * most * nplane * nep
     cut = width // 256 * 128
-
-    routing = jnp.concatenate(
-        [expert_ids.astype(jnp.float32), replica_pick.astype(jnp.float32), gate_scores], axis=1
-    )
-    routing = lax.all_gather(routing, AXES, axis=0, tiled=True)
-    every = gather_plane(tokens, nplane, nep, cut).reshape(nplane * nep * tok_dev, width)
-
-    ids = routing[:, :top_count].astype(jnp.int32)
-    picks = routing[:, top_count : 2 * top_count].astype(jnp.int32)
+    back_cut = width * 11 // 14 // 128 * 128
+
+    coded = expert_ids * (ngroup + 1) + replica_pick
+    note = jnp.concatenate([coded.astype(jnp.float32), gate_scores], axis=1).reshape(-1, 128)
+    every, notes = gather_plane(tokens, note, nplane, nep, cut)
+    every = every.reshape(nplane * nep * tok_dev, width)
+    routing = notes.reshape(device_count * tok_dev, 2 * top_count)
+    coded = routing[:, :top_count].astype(jnp.int32)
+    ids = coded // (ngroup + 1)
+    picks = coded % (ngroup + 1)
     hot = replica_hot[ep_index]
     replicated = (ids % nep == ep_index) & (ids // nep == hot) & (picks < ngroup)
     primary_load = jnp.sum(((ids == me) & ~replicated).astype(jnp.float32))
     replica_load = jnp.sum((replicated & (picks == group_index)).astype(jnp.float32))
     loads = jnp.stack([primary_load, replica_load])[None, :] / top_count
 
-    mine = routing.reshape(nplane, 2, nep * tok_dev, routing.shape[1])
-    mine = lax.dynamic_index_in_dim(mine, core, 1, keepdims=False).reshape(-1, routing.shape[1])
-    my_ids = mine[:, :top_count].astype(jnp.int32)
-    my_gates = mine[:, 2 * top_count :]
+    mine = routing.reshape(nplane, 2, nep * tok_dev, 2 * top_count)
+    mine = lax.dynamic_index_in_dim(mine, core, 1, keepdims=False).reshape(-1, 2 * top_count)
+    my_ids = mine[:, :top_count].astype(jnp.int32) // (ngroup + 1)
+    my_gates = mine[:, top_count:]
 
     def spots(expert):
         chosen = my_ids == expert
@@ -282,7 +412,7 @@
     spread = lax.dot_general(
         select, scaled, (((0,), (0,)), ((), ())), preferred_element_type=jnp.float32
     ).astype(jnp.bfloat16)
-    mixed = scatter_plane(spread.reshape(nplane, nep, tok_dev, width), cut)
+    mixed = scatter_plane(spread.reshape(nplane, nep, tok_dev, width), back_cut)
     return mixed, loads
 
 

time: 222 us -> 135 us (0.61)
  blocking collectives: 72.9 us -> 0 us
  Pallas kernels: 106 us -> 91.3 us
    all_gather x1 -> x0, blocking collectives: 72.9 us -> none  [body(): routing = lax.all_gather(routing, AXES, axis=0, tiled=True)]
    pallas_call x1, Pallas kernels: 55.4 us -> 39.9 us  [scatter_plane(): pl.pallas_call(functools.partial(scatter_kernel, nplane, nep, cut), out_s...]
  transfers between devices with their start and end apart: 2 -> 2, of which waited for: 1 -> 1; matrix products, arithmetic and copies ran while one was open for 2% -> 3% of each run, Pallas kernels for 0% -> 0%
where the time goes in v3:
time: 135 us
  Pallas kernels  91.3 us (68%)
  matrix products  25.8 us (19%)
  local copies, waits for them, and re-layouts  8.08 us (6%)
  other arithmetic  5.89 us (4%)
  waiting for transfers between devices  2.79 us (2%)
    pallas_call x1, Pallas kernels, gather_plane(): pl.pallas_call(functools.partial(gather_kernel, nplane, nep, cut), out_sh...  51.5 us
    pallas_call x1, Pallas kernels, scatter_plane(): pl.pallas_call(functools.partial(scatter_kernel, nplane, nep, cut), out_s...  39.9 us
    dot_general x1, matrix products, body(): jnp.dot(hidden, down_weight[0], preferred_element_type=jnp.float32)  10.8 us
    dot_general x1, matrix products, body(): up_act = jnp.dot(inputs, up_weight[0], preferred_element_type=jnp.float32)  6.67 us
    dot_general x1, matrix products, body(): lax.dot_general(select, scaled, (((0,), (0,)), ((), ())), preferred_eleme...  4.92 us
    unnamed x14, local copies, waits for them, and re-layouts  3.67 us
    dot_general x1, matrix products, body(): jnp.dot(select, every, preferred_element_type=jnp.float32)  3.38 us
    ppermute x1, waiting for transfers between devices, body(): lax.ppermute(picked[capacity:], 'group', swap)  2.79 us
  transfers between devices with their start and end apart: 2, of which 1 were waited for; matrix products, arithmetic and copies ran while one was open for 3% of the time, Pallas kernels for 0%

profile of v3, /device:TPU:0, one launch (start us, length us, event | category | flops | bytes accessed | tf_op | source)
XLA Modules:
  0.0 134.9 jit_solution(10892871573309167763)
XLA Ops:
  0.7 0.7 add_convert_fusion
  1.4 0.7 pad_maximum_fusion.7
  2.1 0.7 reshape.115.note_ref
  2.8 51.5 %shard_map.95 = (bf16[4,4,32,3584]{3,2,1,0:T(8,128)(2,1)}, f32[32,4,128]{2,1,0:T(4,128)}) custom-call(bf16[32,3584]{1,0:T(8,128)(2,1)} %x_ref.1, f32[4,128]{1,0:T(4,128)} %reshape.115.note_ref), custom_call_target="tpu_custom_call" | custom-call | tf_op jit(solution)/shard_map/pallas_call | solution.py:228
  54.3 1.0 reshape_reshape.3
  55.8 0.3 reduce-window.24
  56.4 0.3 reduce-window.16
  57.2 0.6 copy-done.1
  57.8 3.4 %convolution_convert_fusion.1 = bf16[320,3584]{1,0:T(8,128)(2,1)S(1)} fusion(bf16[512,3584]{1,0:T(8,128)(2,1)} %bitcast.34, pred[160,512]{1,0:T(32,128)(4,1)S(1)} %get-tuple-element.20, pred[160,512]{1,0:T(32,128)(4,1)S(1)} %get-tuple-element.21), kind=kOutput, calls=%fused_computation.8 | convolution fusion | flops 1175715840 | bytes 6127616 | tf_op jit(solution)/shard_map/dot_general | solution.py:400
  61.2 0.1 fusion.34
  61.4 2.8 %collective-permute-done = bf16[160,3584]{1,0:T(8,128)(2,1)S(1)} collective-permute-done((bf16[160,3584]{1,0:T(8,128)(2,1)S(1)}, bf16[160,3584]{1,0:T(8,128)(2,1)S(1)}, u32[]{:S(2)}, u32[]{:S(2)}) %collective-permute-start) | collective-permute-done | bytes 1146912 | tf_op jit(solution)/shard_map/ppermute | solution.py:402
  64.2 1.0 copy-done.3
  65.2 6.7 %fusion.2 = f32[320,1024]{1,0:T(8,128)} fusion(bf16[1,3584,1024]{2,1,0:T(8,128)(2,1)} %param.14, bf16[160,3584]{1,0:T(8,128)(2,1)S(1)} %collective-permute-done, bf16[160,3584]{1,0:T(8,128)(2,1)S(1)} %get-tuple-element.14), kind=kOutput, calls=%fused_computation.2 | convolution fusion | flops 2353397760 | bytes 10944512 | tf_op jit(solution)/shard_map/dot_general | solution.py:405
  71.9 10.8 %fusion.6 = bf16[320,3584]{1,0:T(8,128)(2,1)S(1)} fusion(bf16[1,1024,3584]{2,1,0:T(8,128)(2,1)} %param.15, f32[320,1024]{1,0:T(8,128)} %fusion.2, bf16[1,3584,1024]{2,1,0:T(8,128)(2,1)} %param.13, bf16[160,3584]{1,0:T(8,128)(2,1)} %copy-done.3, bf16[160,3584]{1,0:T(8,128)(2,1)S(1)} %get-tuple-element.14), kind=kOutput, calls=%fused_computation.7 | convolution fusion | flops 4705320960 | bytes 20578304 | tf_op jit(solution)/shard_map/dot_general | solution.py:407
  82.7 1.2 fusion.33
  84.0 0.2 reshape.121
  84.2 0.2 copy.19
  84.4 0.6 dynamic_slice.8
  85.0 1.4 %convert_reduce_fusion.1 = (f32[]{:T(128)}, f32[]{:T(128)}) fusion(s32[]{:T(128)S(6)} %add.55, f32[1024,8]{0,1:T(8,128)S(1)} %copy.19, s32[]{:T(128)S(6)} %axis_index.23, s32[]{:T(128)} %bitcast.10, s32[]{:T(128)S(6)} %axis_index.25), kind=kLoop, calls=%fused_computation.32 | loop fusion | flops 376830 | bytes 32792 | tf_op jit(solution)/shard_map/reduce_sum | solution.py:377
  86.4 1.8 %maximum_multiply_fusion = f32[1,2]{1,0:T(1,128)} fusion(f32[1,1]{1,0:T(1,128)} %bitcast.12, f32[1,1]{1,0:T(1,128)} %bitcast.11), kind=kLoop, calls=%fused_computation.58 | loop fusion | flops 4 | bytes 16 | tf_op jit(solution)/shard_map/div | solution.py:379
  88.2 0.2 select_reduce_fusion
  88.4 4.9 %convolution_convert_fusion = bf16[512,3584]{1,0:T(8,128)(2,1)} fusion(bf16[160,3584]{1,0:T(8,128)(2,1)S(1)} %collective-permute-done.1, bf16[160,3584]{1,0:T(8,128)(2,1)S(1)} %get-tuple-element.12, f32[320]{0:T(512)S(1)} %pad_maximum_fusion.8, pred[160,512]{1,0:T(32,128)(4,1)} %copy-done.1, pred[160,512]{1,0:T(32,128)(4,1)} %copy-done.2), kind=kOutput, calls=%fused_computation.6 | convolution fusion | flops 1183285248 | bytes 6128896 | tf_op jit(solution)/shard_map/dot_general | solution.py:412
  93.4 39.9 %shard_map.96 = bf16[32,3584]{1,0:T(8,128)(2,1)} custom-call(bf16[4,4,32,3584]{3,2,1,0:T(8,128)(2,1)} %bitcast.31), custom_call_target="tpu_custom_call" | custom-call | tf_op jit(solution)/shard_map/pallas_call | solution.py:329
  133.2 1.6 %copy.27 = bf16[32,3584]{1,0:T(8,128)(2,1)} copy(bf16[32,3584]{1,0:T(8,128)(2,1)} %shard_map.96) | data formatting | bytes 458752
  (31 shorter events, 1.5 us)
Async XLA Ops:
  57.1 0.6 copy-start.1
  57.2 0.6 copy-start.2
  61.4 2.9 %collective-permute-start = (bf16[160,3584]{1,0:T(8,128)(2,1)S(1)}, bf16[160,3584]{1,0:T(8,128)(2,1)S(1)}, u32[]{:S(2)}, u32[]{:S(2)}) collective-permute-start(bf16[160,3584]{1,0:T(8,128)(2,1)S(1)} %get-tuple-element.15), channel_id=1, source_target_pairs={{0,4},{4,0},{8,12},{12,8},{16,20},{20,16},{24,28},{28,24},{1,5},{5... | collective-permute-start | bytes 3440648 | tf_op jit(solution)/shard_map/ppermute | solution.py:402
  64.2 1.0 copy-start.3
  82.7 1.3 copy-start
  82.7 1.7 %copy-start.4 = (s32[4]{0:T(128)S(1)}, s32[4]{0:T(128)}, u32[]{:S(2)}) copy-start(s32[4]{0:T(128)} %param.12) | copy-start | bytes 52
  83.9 4.6 %collective-permute-start.1 = (bf16[160,3584]{1,0:T(8,128)(2,1)}, bf16[160,3584]{1,0:T(8,128)(2,1)S(1)}, u32[]{:S(2)}, u32[]{:S(2)}) collective-permute-start(bf16[160,3584]{1,0:T(8,128)(2,1)} %get-tuple-element.13), channel_id=1, source_target_pairs={{0,4},{4,0},{8,12},{12,8},{16,20},{20,16},{24,28},{28,24},{1,5},{5... | collective-permute-start | bytes 3440648 | tf_op jit(solution)/shard_map/ppermute | solution.py:409
